TPU v7x, 256 devices: a whole 4x4x8 slice. The times are simulated.
256 devices in a mesh: pq: 32 (over z, x), hh: 8 (over y, core).
Axes of the slice: x: 4, y: 4, z: 8, core: 2. Of those that a mesh axis runs over, the one named last changes fastest.
Arguments:
- amplitudes: bfloat16 [4096, 8192], P('hh', 'pq'), may hold values from -6 to 6
- integrals: bfloat16 [4096, 8192], P('hh', 'pq'), may hold values from -0.0009765625 to 0.0009765625
- left_amps: bfloat16 [8, 4096, 4096], P(None, 'hh', 'pq'), may hold values from -6 to 6
Outputs:
- sigma_ladder: bfloat16 [8, 4096, 4096], P(None, 'hh', 'pq')
- subspace: float32 [8, 8], replicated
All inputs are finite; a program needn't handle non-finite values.
Results may differ from a plain program's by a relative error of at most 0.0049.
Values may be sent and summed in bfloat16 or wider, within the bound.
A program may use at most 64 MiB of HBM per device.

v0:
```python
import math

import jax
import jax.numpy as jnp
from jax import lax
from jax.sharding import Mesh
from jax.sharding import PartitionSpec as P

OCC_PAIRS = 4096
HH = ("hh_0", "hh_1")
PQ = ("pq_0", "pq_1")
PQ_HH = ("pq_0", "pq_1", "hh_0", "hh_1")


def in_order(parts, dim):
    dims = list(parts.shape[1:])
    dims[dim] *= parts.shape[0]
    return jnp.moveaxis(parts, 0, dim).reshape(dims)


def from_everyone(value, axis):
    copies = jnp.broadcast_to(value, (lax.axis_size(axis), *value.shape))
    return lax.all_to_all(copies, axis, split_axis=0, concat_axis=0, tiled=True)


def collect(value, axis, dim):
    return in_order(from_everyone(value, axis), dim)


def scatter_axes(value, axes, dim):
    for axis in axes:
        value = lax.psum_scatter(value, axis, scatter_dimension=dim, tiled=True)
    return value


def gather_axes(value, axes, dim):
    result = value
    for number in range(len(axes) - 1, -1, -1):
        result = lax.all_gather(result, axes[number], axis=dim, tiled=True)
    return result


def one_axis_at_a_time(value, axes):
    for axis in axes:
        value = lax.psum(value, axis)
    return value


def body(amplitudes, integrals, left_amps):
    root_count = left_amps.shape[0]
    ab_cols = left_amps.shape[2]
    partial_t = lax.dot_general(
        integrals,
        collect(amplitudes, HH, 0),
        (((1,), (1,)), ((), ())),
        preferred_element_type=jnp.float32,
    )
    ladder_t = scatter_axes(partial_t, PQ, 1).astype(jnp.bfloat16)
    ladder_t = gather_axes(ladder_t, PQ, 1)
    rows_out = lax.dot_general(
        ladder_t,
        lax.all_gather(left_amps, HH, axis=1, tiled=True),
        (((1,), (1,)), ((), ())),
        preferred_element_type=jnp.float32,
    )
    sigma_out = jnp.transpose(rows_out, (1, 0, 2)).astype(jnp.bfloat16)
    local_gram = jnp.dot(
        left_amps.reshape(root_count, -1),
        sigma_out.reshape(root_count, -1).T,
        preferred_element_type=jnp.float32,
    )
    factor = 1.0 / math.sqrt(OCC_PAIRS * ab_cols * lax.axis_size(PQ))
    subspace = one_axis_at_a_time(local_gram, PQ_HH) * factor
    return (sigma_out, subspace)


def solution(mesh):
    finer = Mesh(mesh.devices.reshape(8, 4, 4, 2), ("pq_0", "pq_1", "hh_0", "hh_1"))
    placed = (P(HH, PQ), P(HH, PQ), P(None, HH, PQ))
    return jax.shard_map(
        body, mesh=finer, in_specs=placed, out_specs=(P(None, HH, PQ), P()), check_vma=False
    )
```

profile of v0, /device:TPU:1, one launch (start us, length us, event | category | flops | bytes accessed | tf_op | source)
XLA Modules:
  0.0 309.5 jit_solution(8153977485617242432)
XLA Ops:
  8.0 0.0 reduce-scatter.3.cloned.1.call-start
  8.1 1.1 broadcast_in_dim.3
  9.2 31.9 %all_to_all.5 = bf16[8,512,256]{2,1,0:T(8,128)(2,1)S(1)} all-to-all(bf16[8,512,256]{2,1,0:T(8,128)(2,1)S(1)} %broadcast_in_dim.3), channel_id=1, replica_groups=mesh['pq_0'=8,'pq_1'=4,'hh_0'=4,'hh_1'=2] {'hh_0','hh_1'}, dimensions={0} | all-to-all | bytes 4194304 | tf_op jit(solution)/shard_map/all_to_all | solution.py:23
  41.1 4.5 %fusion.10 = f32[512,4096]{1,0:T(8,128)} fusion(bf16[512,256]{1,0:T(8,128)(2,1)S(1)} %copy-done, bf16[4096,256]{1,0:T(8,128)(2,1)S(1)} %bitcast.17), kind=kOutput, calls=%fused_computation.8 | convolution fusion | flops 1073741824 | bytes 10747904 | tf_op jit(solution)/shard_map/dot_general | solution.py:52
  45.6 0.0 reduce-scatter.3.cloned.1.call-update
  45.7 0.0 reduce-scatter.5.cloned.1.call-start
  45.7 96.3 %reduce-scatter.3.cloned.1.call-done = f32[512,512]{1,0:T(8,128)} async-done(((f32[512,4096]{1,0:T(8,128)}), f32[512,512]{1,0:T(8,128)}) %reduce-scatter.3.cloned.1.call-update) | async-done | bytes 1048592 | tf_op jit(solution)/shard_map/reduce_scatter | solution.py:32
  142.0 0.0 reduce-scatter.5.cloned.1.call-update
  142.0 0.0 all-gather.5.cloned.1.call-start
  142.0 0.5 all-gather.5.cloned.1.call-update
  142.6 0.0 all-gather.3.cloned.1.call-start
  142.6 25.4 %reduce-scatter.5.cloned.1.call-done = f32[512,128]{1,0:T(8,128)} async-done(((f32[512,512]{1,0:T(8,128)}), f32[512,128]{1,0:T(8,128)}) %reduce-scatter.5.cloned.1.call-update) | async-done | bytes 262160 | tf_op jit(solution)/shard_map/reduce_scatter | solution.py:32
  168.0 1.0 convert_element_type.9
  169.0 11.7 %all_gather.9 = bf16[512,512]{1,0:T(8,128)(2,1)} all-gather(bf16[512,128]{1,0:T(8,128)(2,1)S(1)} %convert_element_type.9), channel_id=1, replica_groups=mesh['pq_0'=8,'pq_1'=4,'hh_0'=4,'hh_1'=2] {'pq_1'}, dimensions={1}, use_global_device_ids=true | all-gather | bytes 655360 | tf_op jit(solution)/shard_map/all_gather | solution.py:39
  180.7 0.0 all-gather.3.cloned.1.call-update
  180.7 14.8 %all-gather.5.cloned.1.call-done = bf16[8,4096,128]{2,1,0:T(8,128)(2,1)} async-done(((bf16[8,512,128]{2,1,0:T(8,128)(2,1)}), bf16[8,4096,128]{2,1,0:T(8,128)(2,1)}) %all-gather.5.cloned.1.call-update) | async-done | bytes 8388624 | tf_op jit(solution)/shard_map/all_gather | solution.py:62
  195.6 56.0 %all-gather.3.cloned.1.call-done = bf16[512,4096]{1,0:T(8,128)(2,1)} async-done(((bf16[512,512]{1,0:T(8,128)(2,1)}), bf16[512,4096]{1,0:T(8,128)(2,1)}) %all-gather.3.cloned.1.call-update) | async-done | bytes 4194320 | tf_op jit(solution)/shard_map/all_gather | solution.py:39
  251.5 9.1 %fusion.5 = bf16[8,512,128]{2,1,0:T(8,128)(2,1)S(1)} fusion(bf16[8,4096,128]{2,1,0:T(8,128)(2,1)} %all-gather.5.cloned.1.call-done, bf16[512,4096]{1,0:T(8,128)(2,1)} %all-gather.3.cloned.1.call-done), kind=kOutput, calls=%fused_computation.3 | convolution fusion | flops 4295491584 | bytes 13631488 | tf_op jit(solution)/shard_map/dot_general | solution.py:60
  260.7 1.3 convolution_bitcast_fusion
  262.0 11.8 %psum.28 = f32[8,8]{0,1:T(8,128)S(1)} all-reduce(f32[8,8]{0,1:T(8,128)S(1)} %convolution_bitcast_fusion), channel_id=1, replica_groups=mesh['pq_0'=8,'pq_1'=4,'hh_0'=4,'hh_1'=2] {'pq_0'}, use_global_device_ids=true, to_apply=%region_2.0 | all-reduce | flops 64 | bytes 512 | tf_op jit(solution)/shard_map/psum | solution.py:45
  273.8 8.4 %psum.29 = f32[8,8]{0,1:T(8,128)S(1)} all-reduce(f32[8,8]{0,1:T(8,128)S(1)} %psum.28), channel_id=1, replica_groups=mesh['pq_0'=8,'pq_1'=4,'hh_0'=4,'hh_1'=2] {'pq_1'}, use_global_device_ids=true, to_apply=%region_3.0 | all-reduce | flops 64 | bytes 512 | tf_op jit(solution)/shard_map/psum | solution.py:45
  282.2 8.4 %psum.30 = f32[8,8]{0,1:T(8,128)S(1)} all-reduce(f32[8,8]{0,1:T(8,128)S(1)} %psum.29), channel_id=1, replica_groups=mesh['pq_0'=8,'pq_1'=4,'hh_0'=4,'hh_1'=2] {'hh_0'}, use_global_device_ids=true, to_apply=%region_4.0 | all-reduce | flops 64 | bytes 512 | tf_op jit(solution)/shard_map/psum | solution.py:45
  290.6 10.8 %psum.31 = f32[8,8]{0,1:T(8,128)S(1)} all-reduce(f32[8,8]{0,1:T(8,128)S(1)} %psum.30), channel_id=1, replica_groups=mesh['pq_0'=8,'pq_1'=4,'hh_0'=4,'hh_1'=2] {'hh_1'}, use_global_device_ids=true, to_apply=%region_5.0 | all-reduce | flops 64 | bytes 512 | tf_op jit(solution)/shard_map/psum | solution.py:45
  301.4 0.7 copy.7
  (7 shorter events, 0.0 us)
Async XLA Ops:
  8.0 33.1 %copy-start = (bf16[512,256]{1,0:T(8,128)(2,1)S(1)}, bf16[512,256]{1,0:T(8,128)(2,1)}, u32[]{:S(2)}) copy-start(bf16[512,256]{1,0:T(8,128)(2,1)} %param.4) | copy-start | bytes 786436
  8.0 134.0 %reduce-scatter.3.cloned.1.call-start = ((), (), s32[]{:S(2)}) async-start(), calls=%async_computation.3 | async-start | bytes 9437184 | tf_op jit(solution)/shard_map/reduce_scatter | solution.py:32
  45.7 122.4 %reduce-scatter.5.cloned.1.call-start = ((), (), s32[]{:S(2)}) async-start(), calls=%async_computation.4 | async-start | bytes 1310720 | tf_op jit(solution)/shard_map/reduce_scatter | solution.py:32
  142.0 53.6 %all-gather.5.cloned.1.call-start = ((), (), s32[]{:S(2)}) async-start(), calls=%async_computation.6 | async-start | bytes 9437184 | tf_op jit(solution)/shard_map/all_gather | solution.py:62
  142.6 108.9 %all-gather.3.cloned.1.call-start = ((), (), s32[]{:S(2)}) async-start(), calls=%async_computation.5 | async-start | bytes 4718592 | tf_op jit(solution)/shard_map/all_gather | solution.py:39
  180.7 80.0 %copy-start.1 = (bf16[8,512,128]{2,1,0:T(8,128)(2,1)S(1)}, bf16[8,512,128]{2,1,0:T(8,128)(2,1)}, u32[]{:S(2)}) copy-start(bf16[8,512,128]{2,1,0:T(8,128)(2,1)} %param.5) | copy-start | bytes 3145732
  260.7 41.4 %copy-start.2 = (bf16[8,512,128]{2,1,0:T(8,128)(2,1)}, bf16[8,512,128]{2,1,0:T(8,128)(2,1)S(1)}, u32[]{:S(2)}) copy-start(bf16[8,512,128]{2,1,0:T(8,128)(2,1)S(1)} %fusion.5) | copy-start | bytes 3145732
Sparse Core Ops, SparseCore 0:
  45.8 96.1 reduce-scatter.2
  144.5 23.4 reduce-scatter.4
Sparse Core Ops, SparseCore 1:
  144.3 51.2 all-gather.4
  197.2 54.2 all-gather.2
where the time goes:
time: 310 us
  waiting for transfers between devices  193 us (62%)
  blocking collectives  83 us (27%)
  between operations  15.5 us (5%)
  matrix products  15 us (5%)
    reduce_scatter x2, waiting for transfers between devices, scatter_axes(): value = lax.psum_scatter(value, axis, scatter_dimension=dim, tiled=True)  122 us
    all_gather x1, waiting for transfers between devices, gather_axes(): result = lax.all_gather(result, axes[number], axis=dim, tiled=True)  56 us
    psum x4, blocking collectives, one_axis_at_a_time(): value = lax.psum(value, axis)  39.4 us
    all_to_all x1, blocking collectives, from_everyone(): return lax.all_to_all(copies, axis, split_axis=0, concat_axis=0, tiled=True)  31.9 us
    all_gather x1, waiting for transfers between devices, body(): lax.all_gather(left_amps, HH, axis=1, tiled=True)  14.8 us
    all_gather x1, blocking collectives, gather_axes(): result = lax.all_gather(result, axes[number], axis=dim, tiled=True)  11.7 us
    dot_general x1, matrix products, body(): lax.dot_general(ladder_t, lax.all_gather(left_amps, HH, axis=1, tiled=Tru...  9.14 us
  transfers between devices with their start and end apart: 4, of which 4 were waited for; matrix products, arithmetic and copies ran while one was open for 0% of the time, Pallas kernels for 0%

commit v1 on v0

v1 whole, which is shorter than its diff:
```python
import functools
import math

import jax
import jax.numpy as jnp
from jax import lax
from jax.experimental import pallas as pl
from jax.experimental.pallas import tpu as pltpu
from jax.sharding import Mesh
from jax.sharding import PartitionSpec as P

MESH = pl.DeviceIdType.MESH
AXES = ("z", "x", "y", "core")
CHUNKS = 2
NT = (((1,), (1,)), ((), ()))


def messages(nz):
    far = nz // 2
    names = [("a", dx) for dx in (1, 2, 3)]
    names += [("i", sign, half) for sign in (1, -1) for half in (0, 1, 2)]
    for dx in range(4):
        names += [("t", dx, sign, kind) for sign in (1, -1) for kind in ("own", "fwd")]
        names += [("tc", dx, dy) for dy in range(4)]
    for k in range(CHUNKS):
        for sign, length in chains(k, far):
            names += [("r", k, sign, s) for s in range(1, length + 1)]
    names += [("l", sign, half) for sign in (1, -1) for half in (0, 1, 2)]
    names += [("lc", 0)] + [("lc", dy, half) for dy in (1, 2, 3) for half in (0, 1)]
    names += [("ax", sign, kind) for sign in (1, -1) for kind in ("own", "fwd")]
    names += [("az", dx, sign, s) for dx in range(4) for sign in (1, -1) for s in range(1, far + 1)]
    names += [("bz", sign, s) for sign in (1, -1) for s in range(1, far + 1)]
    names += [("bx", dz, sign, kind) for dz in range(nz) for sign in (1, -1) for kind in ("own", "fwd")]
    return {name: number for number, name in enumerate(names)}


def chains(k, far):
    return ((1, far), (-1, far - 1)) if k % 2 == 0 else ((-1, far), (1, far - 1))


def kernel(ids, nz, t2_hbm, int_hbm, left_hbm, out_ref, gram_ref,
           t2x, ints, part, rs_send, rs_recv, lad, left, acc, send_sem, recv_sem, local_sem):
    far = nz // 2
    size = {"z": nz, "x": 4, "y": 4, "core": 2}
    pos = {axis: lax.axis_index(axis) for axis in AXES}
    z, x, y, core = (pos[axis] for axis in AXES)
    quarter = t2x.shape[2]
    rows = lad.shape[2]
    a_rows = rows * 3 // 8
    a_span = (0, a_rows)
    b_span = (a_rows, rows - a_rows)

    def step(axis, offset):
        return lax.rem(pos[axis] + (offset + size[axis]), size[axis])

    def hidx(dy):
        return step("y", dy) * 2 + core

    h_me = y * 2 + core
    sent = []
    posted = set()

    def post(name, axis, offset, src, dst):
        k = ids[name]
        copy = pltpu.make_async_remote_copy(
            src_ref=src, dst_ref=dst, send_sem=send_sem.at[k], recv_sem=recv_sem.at[k],
            device_id={axis: step(axis, offset)}, device_id_type=MESH)
        copy.start()
        sent.append(copy)
        posted.add(name)

    def await_(name, dst):
        assert name in posted
        posted.remove(name)
        k = ids[name]
        pltpu.make_async_remote_copy(
            src_ref=dst, dst_ref=dst, send_sem=send_sem.at[k], recv_sem=recv_sem.at[k],
            device_id={"core": 1 - core}, device_id_type=MESH).wait_recv()

    own_t2 = pltpu.make_async_copy(
        t2_hbm.at[pl.ds(pl.multiple_of(x * quarter, quarter), quarter)], t2x.at[h_me, x], local_sem.at[0])
    own_int = pltpu.make_async_copy(int_hbm, ints.at[x], local_sem.at[1])
    own_left = pltpu.make_async_copy(left_hbm, left.at[h_me], local_sem.at[2])
    own_t2.start()
    own_int.start()
    own_left.start()

    barrier = pltpu.get_barrier_semaphore()
    near = (("x", 1), ("x", 2), ("x", 3), ("y", 1), ("y", 3), ("z", 1), ("z", -1), ("core", 1))
    for axis, offset in near:
        pl.semaphore_signal(barrier, inc=1, device_id={axis: step(axis, offset)}, device_id_type=MESH)
    pl.semaphore_wait(barrier, len(near))

    for dx in (2, 1, 3):
        to = step("x", dx)
        post(("a", dx), "x", dx,
             t2_hbm.at[pl.ds(pl.multiple_of(to * quarter, quarter), quarter)], t2x.at[h_me, x])
    half = rows // 2
    for sign in (1, -1):
        for n, part_no in enumerate((0, 1) if sign == 1 else (1, 0)):
            post(("i", sign, n), "x", sign,
                 int_hbm.at[pl.ds(part_no * half, half)], ints.at[x, pl.ds(part_no * half, half)])

    def t2_piece(dx):
        xi = step("x", dx)
        block = t2x.at[h_me, xi]
        for sign in (1, -1):
            post(("t", dx, sign, "own"), "y", sign, block, block)
        post(("tc", dx, 0), "core", 1, block, block)

    def t2_near(dx):
        xi = step("x", dx)
        for sign in (1, -1):
            block = t2x.at[hidx(-sign), xi]
            await_(("t", dx, sign, "own"), block)
            lo = 0 if sign == 1 else quarter // 2
            piece = t2x.at[hidx(-sign), xi, pl.ds(lo, quarter // 2)]
            post(("t", dx, sign, "fwd"), "y", sign, piece, piece)
            post(("tc", dx, -sign % 4), "core", 1, block, block)

    def t2_far(dx):
        xi = step("x", dx)
        for sign in (1, -1):
            lo = 0 if sign == 1 else quarter // 2
            await_(("t", dx, sign, "fwd"), t2x.at[hidx(2), xi, pl.ds(lo, quarter // 2)])
        block = t2x.at[hidx(2), xi]
        post(("tc", dx, 2), "core", 1, block, block)

    def int_near():
        for sign in (1, -1):
            part_no = 0 if sign == 1 else 1
            block = ints.at[step("x", -sign), pl.ds(part_no * half, half)]
            await_(("i", sign, 0), block)
            post(("i", sign, 2), "x", sign, block, block)

    own_t2.wait()
    t2_piece(0)
    for dx in (3, 1, 2):
        await_(("a", 4 - dx), t2x.at[h_me, step("x", dx)])
        t2_piece(dx)
    for dx in (0, 3):
        t2_near(dx)
    int_near()
    for dx in (1, 2):
        t2_near(dx)
    own_left.wait()
    root_half = left.shape[1] // 2
    for sign in (1, -1):
        for n, part_no in enumerate((0, 1) if sign == 1 else (1, 0)):
            block = left.at[h_me, pl.ds(part_no * root_half, root_half)]
            post(("l", sign, n), "y", sign, block, block)
    for dx in (0, 3, 1, 2):
        t2_far(dx)
    post(("lc", 0), "core", 1, left.at[h_me], left.at[h_me])
    own_int.wait()
    for sign in (1, -1):
        part_no = 1 if sign == 1 else 0
        await_(("i", sign, 1), ints.at[step("x", -sign), pl.ds(part_no * half, half)])
    for sign in (1, -1):
        part_no = 0 if sign == 1 else 1
        await_(("i", sign, 2), ints.at[step("x", 2), pl.ds(part_no * half, half)])
    for dx in (0, 3, 1, 2):
        for dy in range(4):
            await_(("tc", dx, dy), t2x.at[step("y", dy) * 2 + (1 - core), step("x", dx)])

    def partial(d):
        total = lax.dot_general(ints[0], t2x[d, 0], NT, preferred_element_type=jnp.float32)
        for xi in range(1, 4):
            total += lax.dot_general(ints[xi], t2x[d, xi], NT, preferred_element_type=jnp.float32)
        part[d] = total

    chunk = rows // CHUNKS

    def rs_step(k, sign, length, s):
        d = step("z", sign * (length + 1 - s))
        lane = 0 if sign == 1 else 1
        value = part[d, pl.ds(k * chunk, chunk)]
        if s > 1:
            await_(("r", k, sign, s - 1), rs_recv.at[k, lane, s - 2])
            value += rs_recv[k, lane, s - 2].astype(jnp.float32)
        rs_send[k, lane, s - 1] = value.astype(jnp.bfloat16)
        post(("r", k, sign, s), "z", sign, rs_send.at[k, lane, s - 1], rs_recv.at[k, lane, s - 1])

    partial(step("z", far))
    for k in range(CHUNKS):
        sign, length = chains(k, far)[0]
        rs_step(k, sign, length, 1)
    partial(step("z", far - 1))
    partial(step("z", 1 - far))
    for k in range(CHUNKS):
        sign, length = chains(k, far)[1]
        rs_step(k, sign, length, 1)

    def rest(i, carry):
        partial(lax.rem(z + (nz - far + 2) + i, nz))
        return carry

    lax.fori_loop(0, nz - 3, rest, 0)
    for s in range(2, far + 1):
        for which in (0, 1):
            for k in range(CHUNKS):
                sign, length = chains(k, far)[which]
                if s <= length:
                    rs_step(k, sign, length, s)
    for k in range(CHUNKS):
        value = part[z, pl.ds(k * chunk, chunk)]
        for sign, length in chains(k, far):
            lane = 0 if sign == 1 else 1
            await_(("r", k, sign, length), rs_recv.at[k, lane, length - 1])
            value += rs_recv[k, lane, length - 1].astype(jnp.float32)
        lad[z, x, pl.ds(k * chunk, chunk)] = value.astype(jnp.bfloat16)

    def cut(span, which):
        lo, count = span
        if which is None:
            return pl.ds(lo, count)
        return pl.ds(lo + which * (count // 2), count // 2)

    def lad_at(dz, dx, span, which=None):
        return lad.at[step("z", dz), step("x", dx), cut(span, which)]

    def along_x(tag, dz, span, dx_own=0):
        block = lad_at(dz, 0, span)
        for sign in (1, -1):
            post(tag + (sign, "own"), "x", sign, block, block)

    def x_near(tag, dz, span, sign):
        await_(tag + (sign, "own"), lad_at(dz, -sign, span))
        which = 0 if sign == 1 else 1
        piece = lad_at(dz, -sign, span, which)
        post(tag + (sign, "fwd"), "x", sign, piece, piece)

    def x_far(tag, dz, span):
        for sign in (1, -1):
            await_(tag + (sign, "fwd"), lad_at(dz, 2, span, 0 if sign == 1 else 1))

    def along_z(tag, dx, span):
        block = lad_at(0, dx, span)
        for sign in (1, -1):
            post(tag + (sign, 1), "z", sign, block, block)

    def z_hop(tag, dx, span, sign, s):
        which = 0 if sign == 1 else 1
        if s < far:
            await_(tag + (sign, s), lad_at(-sign * s, dx, span))
            block = lad_at(-sign * s, dx, span, which if s + 1 == far else None)
            post(tag + (sign, s + 1), "z", sign, block, block)
        else:
            await_(tag + (sign, s), lad_at(far, dx, span, which))

    def left_near():
        for sign in (1, -1):
            part_no = 0 if sign == 1 else 1
            block = left.at[hidx(-sign), pl.ds(part_no * root_half, root_half)]
            await_(("l", sign, 0), block)
            post(("l", sign, 2), "y", sign, block, block)
            post(("lc", -sign % 4, part_no), "core", 1, block, block)

    def left_second():
        for sign in (1, -1):
            part_no = 1 if sign == 1 else 0
            block = left.at[hidx(-sign), pl.ds(part_no * root_half, root_half)]
            await_(("l", sign, 1), block)
            post(("lc", -sign % 4, part_no), "core", 1, block, block)

    def left_far():
        for sign in (1, -1):
            part_no = 0 if sign == 1 else 1
            block = left.at[hidx(2), pl.ds(part_no * root_half, root_half)]
            await_(("l", sign, 2), block)
            post(("lc", 2, part_no), "core", 1, block, block)

    def left_partner():
        other = 1 - core
        await_(("lc", 0), left.at[y * 2 + other])
        for dy in (1, 3, 2):
            for part_no in (0, 1):
                await_(("lc", dy, part_no),
                       left.at[step("y", dy) * 2 + other, pl.ds(part_no * root_half, root_half)])

    def sigma_row(dz, first):
        h = step("z", dz)
        lhs = jnp.concatenate([lad[h, xi] for xi in range(4)], axis=1)

        def pair(j, carry):
            rhs = jnp.concatenate([left[h, 2 * j], left[h, 2 * j + 1]], axis=1)
            value = jnp.dot(lhs, rhs, preferred_element_type=jnp.float32)
            if first:
                acc[j] = value
            else:
                acc[j] += value
            return carry

        lax.fori_loop(0, acc.shape[0], pair, 0)

    along_z(("bz",), 0, b_span)
    along_x(("ax",), 0, a_span)
    along_z(("az", 0), 0, a_span)
    along_x(("bx", 0), 0, b_span)
    left_near()
    for r in range(1, far + 3):
        if r < far:
            for sign in (1, -1):
                z_hop(("bz",), 0, b_span, sign, r)
                dz = -sign * r
                along_x(("bx", dz % nz), dz, b_span)
        elif r == far:
            for sign in (1, -1):
                z_hop(("bz",), 0, b_span, sign, r)
            along_x(("bx", far), far, b_span)
        if r == 1:
            for sign in (1, -1):
                x_near(("ax",), 0, a_span, sign)
                along_z(("az", -sign % 4), -sign, a_span)
        if r == 2:
            x_far(("ax",), 0, a_span)
            along_z(("az", 2), 2, a_span)
        for dx in (0, 3, 1, 2):
            s = r - min(dx, 4 - dx)
            if 1 <= s <= far:
                for sign in (1, -1):
                    z_hop(("az", dx), dx, a_span, sign, s)
        for dz in sorted({(sign * (r - 1)) % nz for sign in (1, -1)}) if r - 1 <= far else ():
            for sign in (1, -1):
                x_near(("bx", dz), dz, b_span, sign)
        for dz in sorted({(sign * (r - 2)) % nz for sign in (1, -1)}) if 0 <= r - 2 <= far else ():
            x_far(("bx", dz), dz, b_span)
        if r == far - 1:
            left_second()
        if r == far:
            left_far()
        if r == far + 1:
            left_partner()
            for n, dz in enumerate(sorted({sign * q for q in range(far) for sign in (1, -1)}, key=abs)):
                sigma_row(dz, n == 0)
    sigma_row(far, False)

    roots = out_ref.shape[0]
    cols = out_ref.shape[2]

    def finish(j, carry):
        for i in range(2):
            s = 2 * j + i
            rounded = acc[j, :, i * cols:(i + 1) * cols].astype(jnp.bfloat16)
            out_ref[s] = rounded
            wide = rounded.astype(jnp.float32)
            lines = [jnp.sum(left[h_me, r].astype(jnp.float32) * wide, axis=0, keepdims=True)
                     for r in range(roots)]
            gram_ref[s] = jnp.concatenate(lines, axis=0)
        return carry

    lax.fori_loop(0, roots // 2, finish, 0)
    assert not posted
    for copy in sent:
        copy.wait_send()


def body(nz, amplitudes, integrals, left_amps):
    roots, rows, cols = left_amps.shape
    window = amplitudes.shape[1]
    quarter = rows // 4
    ids = messages(nz)
    far = nz // 2
    any_ = pl.BlockSpec(memory_space=pl.ANY)
    vmem = pl.BlockSpec(memory_space=pltpu.VMEM)
    sigma, gram = pl.pallas_call(
        functools.partial(kernel, ids, nz),
        out_shape=(
            jax.ShapeDtypeStruct((roots, rows, cols), jnp.bfloat16),
            jax.ShapeDtypeStruct((roots, roots, cols), jnp.float32),
        ),
        in_specs=[any_] * 3,
        out_specs=(vmem, vmem),
        scratch_shapes=[
            pltpu.VMEM((8, 4, quarter, window), jnp.bfloat16),
            pltpu.VMEM((4, rows, window), jnp.bfloat16),
            pltpu.VMEM((nz, rows, quarter), jnp.float32),
            pltpu.VMEM((CHUNKS, 2, far, rows // CHUNKS, quarter), jnp.bfloat16),
            pltpu.VMEM((CHUNKS, 2, far, rows // CHUNKS, quarter), jnp.bfloat16),
            pltpu.VMEM((nz, 4, rows, quarter), jnp.bfloat16),
            pltpu.VMEM((8, roots, rows, cols), jnp.bfloat16),
            pltpu.VMEM((roots // 2, rows, 2 * cols), jnp.float32),
            pltpu.SemaphoreType.DMA((len(ids),)),
            pltpu.SemaphoreType.DMA((len(ids),)),
            pltpu.SemaphoreType.DMA((3,)),
        ],
        compiler_params=pltpu.CompilerParams(
            collective_id=0, has_side_effects=True, vmem_limit_bytes=50 * 1024 * 1024),
    )(amplitudes, integrals, left_amps)
    local = jnp.sum(gram, axis=2).T
    occ = rows * 8
    factor = 1.0 / math.sqrt(occ * cols * nz * 4)
    return sigma, lax.psum(local, AXES) * factor


def solution(mesh):
    nz = mesh.devices.size // 32
    finer = Mesh(mesh.devices.reshape(nz, 4, 4, 2), AXES)
    placed = P(("y", "core"), ("z", "x"))
    wide = P(None, ("y", "core"), ("z", "x"))
    return jax.shard_map(
        functools.partial(body, nz), mesh=finer, in_specs=(placed, placed, wide), out_specs=(wide, P()), check_vma=False
    )
```

time: 310 us -> 161 us (0.52)
  waiting for transfers between devices: 193 us -> 0 us
  Pallas kernels: 0 us -> 80.7 us
  matrix products: 15 us -> 0 us
  between operations: 15.5 us -> 0.65 us
  blocking collectives: 83 us -> 75 us
    reduce_scatter x2 -> x0, waiting for transfers between devices: 122 us -> none  [scatter_axes(): value = lax.psum_scatter(value, axis, scatter_dimension=dim, tiled=True)]
    pallas_call x0 -> x1, Pallas kernels: none -> 80.7 us  [body(): pl.pallas_call(functools.partial(kernel, ids, nz), out_shape=(jax.ShapeDt...]
    all_gather x2 -> x0, waiting for transfers between devices: 70.8 us -> none  [the longest x1 56 us: gather_axes(): result = lax.all_gather(result, axes[number], axis=dim, tiled=True)]
    psum x4 -> x1, blocking collectives: 39.4 us -> 75 us  [body(): return (sigma, lax.psum(local, AXES) * factor)]
    all_to_all x1 -> x0, blocking collectives: 31.9 us -> none  [from_everyone(): return lax.all_to_all(copies, axis, split_axis=0, concat_axis=0, tiled=True)]
    dot_general x3 -> x0, matrix products: 15 us -> none  [the longest x1 9.14 us: body(): lax.dot_general(ladder_t, lax.all_gather(left_amps, HH, axis=1, tiled=Tru...]
    all_gather x1 -> x0, blocking collectives: 11.7 us -> none  [gather_axes(): result = lax.all_gather(result, axes[number], axis=dim, tiled=True)]
    unnamed x7 -> x8, local copies, waits for them, and re-layouts: 0.69 us -> 4.75 us
  transfers between devices with their start and end apart: 4 -> 0, of which waited for: 4 -> 0; matrix products, arithmetic and copies ran while one was open for 0% -> 0% of each run, Pallas kernels for 0% -> 0%
where the time goes in v1:
time: 161 us
  Pallas kernels  80.7 us (50%)
  blocking collectives  75 us (47%)
  local copies, waits for them, and re-layouts  4.75 us (3%)
    pallas_call x1, Pallas kernels, body(): pl.pallas_call(functools.partial(kernel, ids, nz), out_shape=(jax.ShapeDt...  80.7 us
    psum x1, blocking collectives, body(): return (sigma, lax.psum(local, AXES) * factor)  75 us
    unnamed x8, local copies, waits for them, and re-layouts  4.75 us

profile of v1, /device:TPU:1, one launch (start us, length us, event | category | flops | bytes accessed | tf_op | source)
XLA Modules:
  0.0 161.2 jit_solution(5492671582834155361)
XLA Ops:
  0.6 0.0 copy-start
  0.6 1.2 copy-done
  1.9 0.0 copy-start.1
  1.9 0.9 copy-done.1
  2.8 0.0 copy-start.2
  2.8 0.9 copy-done.2
  3.8 80.7 %shard_map.50 = (bf16[8,512,128]{2,1,0:T(8,128)(2,1)S(1)}, f32[8,8,128]{2,1,0:T(8,128)S(1)}) custom-call(bf16[512,256]{1,0:T(8,128)(2,1)S(1)} %copy-done.1, bf16[512,256]{1,0:T(8,128)(2,1)S(1)} %copy-done.2, bf16[8,512,128]{2,1,0:T(8,128)(2,1)S(1)} %copy-done), custom_call_target="tpu_custom_call" | custom-call | tf_op jit(solution)/shard_map/pallas_call | solution.py:366
  84.5 0.1 reduce_sum.9
  84.6 75.0 %psum.7 = f32[8,8]{0,1:T(8,128)S(1)} all-reduce(f32[8,8]{0,1:T(8,128)S(1)} %bitcast.1), channel_id=1, replica_groups=mesh['z'=8,'x'=4,'y'=4,'core'=2] {'z','x','y','core'}, use_global_device_ids=true, to_apply=%region_1.0 | all-reduce | flops 64 | bytes 512 | tf_op jit(solution)/shard_map/psum | solution.py:393
  159.6 0.7 copy.5
  160.2 1.0 copy.7
  (1 shorter events, 0.0 us)
Async XLA Ops:
  0.6 1.2 copy-start
  1.9 0.9 copy-start.1
  2.8 0.9 copy-start.2

commit v2 on v1

--- a/solution.py
+++ b/solution.py
@@ -31,6 +31,8 @@
     names += [("az", dx, sign, s) for dx in range(4) for sign in (1, -1) for s in range(1, far + 1)]
     names += [("bz", sign, s) for sign in (1, -1) for s in range(1, far + 1)]
     names += [("bx", dz, sign, kind) for dz in range(nz) for sign in (1, -1) for kind in ("own", "fwd")]
+    names += [("gc", dy, dc) for dy in range(4) for dc in (0, 1) if dy or dc]
+    names += [("gx", dx) for dx in (1, 2, 3)] + [("gz", dz) for dz in range(1, nz)]
     return {name: number for number, name in enumerate(names)}
 
 
@@ -39,7 +41,7 @@
 
 
 def kernel(ids, nz, t2_hbm, int_hbm, left_hbm, out_ref, gram_ref,
-           t2x, ints, part, rs_send, rs_recv, lad, left, acc, send_sem, recv_sem, local_sem):
+           t2x, ints, part, rs_send, rs_recv, lad, left, acc, gram_y, gram_x, gram_z, send_sem, recv_sem, local_sem):
     far = nz // 2
     size = {"z": nz, "x": 4, "y": 4, "core": 2}
     pos = {axis: lax.axis_index(axis) for axis in AXES}
@@ -61,10 +63,13 @@
     posted = set()
 
     def post(name, axis, offset, src, dst):
+        post_to(name, {axis: step(axis, offset)}, src, dst)
+
+    def post_to(name, device, src, dst):
         k = ids[name]
         copy = pltpu.make_async_remote_copy(
             src_ref=src, dst_ref=dst, send_sem=send_sem.at[k], recv_sem=recv_sem.at[k],
-            device_id={axis: step(axis, offset)}, device_id_type=MESH)
+            device_id=device, device_id_type=MESH)
         copy.start()
         sent.append(copy)
         posted.add(name)
@@ -338,7 +343,9 @@
     roots = out_ref.shape[0]
     cols = out_ref.shape[2]
 
-    def finish(j, carry):
+    lane = lax.broadcasted_iota(jnp.int32, (roots, 128), 1)
+
+    def finish(j, tile):
         for i in range(2):
             s = 2 * j + i
             rounded = acc[j, :, i * cols:(i + 1) * cols].astype(jnp.bfloat16)
@@ -346,10 +353,37 @@
             wide = rounded.astype(jnp.float32)
             lines = [jnp.sum(left[h_me, r].astype(jnp.float32) * wide, axis=0, keepdims=True)
                      for r in range(roots)]
-            gram_ref[s] = jnp.concatenate(lines, axis=0)
-        return carry
-
-    lax.fori_loop(0, roots // 2, finish, 0)
+            column = jnp.sum(jnp.concatenate(lines, axis=0), axis=1, keepdims=True)
+            tile = jnp.where(lane == s, column, tile)
+        return tile
+
+    tile = lax.fori_loop(0, roots // 2, finish, jnp.zeros((roots, 128), jnp.float32))
+
+    def total(ref):
+        value = ref[0]
+        for n in range(1, ref.shape[0]):
+            value += ref[n]
+        return value
+
+    gram_y[h_me] = tile
+    pairs = [(dy, dc) for dy in (2, 1, 3, 0) for dc in (1, 0) if dy or dc]
+    for dy, dc in pairs:
+        post_to(("gc", dy, dc), {"y": step("y", dy), "core": step("core", dc)},
+                gram_y.at[h_me], gram_y.at[h_me])
+    for dy, dc in pairs:
+        await_(("gc", dy, dc), gram_y.at[step("y", -dy) * 2 + step("core", -dc)])
+    gram_x[x] = total(gram_y)
+    for dx in (2, 1, 3):
+        post(("gx", dx), "x", dx, gram_x.at[x], gram_x.at[x])
+    for dx in (2, 1, 3):
+        await_(("gx", dx), gram_x.at[step("x", -dx)])
+    gram_z[z] = total(gram_x)
+    hops = sorted(range(1, nz), key=lambda dz: -min(dz, nz - dz))
+    for dz in hops:
+        post(("gz", dz), "z", dz, gram_z.at[z], gram_z.at[z])
+    for dz in hops:
+        await_(("gz", dz), gram_z.at[step("z", -dz)])
+    gram_ref[...] = total(gram_z)
     assert not posted
     for copy in sent:
         copy.wait_send()
@@ -367,7 +401,7 @@
         functools.partial(kernel, ids, nz),
         out_shape=(
             jax.ShapeDtypeStruct((roots, rows, cols), jnp.bfloat16),
-            jax.ShapeDtypeStruct((roots, roots, cols), jnp.float32),
+            jax.ShapeDtypeStruct((roots, 128), jnp.float32),
         ),
         in_specs=[any_] * 3,
         out_specs=(vmem, vmem),
@@ -380,17 +414,19 @@
             pltpu.VMEM((nz, 4, rows, quarter), jnp.bfloat16),
             pltpu.VMEM((8, roots, rows, cols), jnp.bfloat16),
             pltpu.VMEM((roots // 2, rows, 2 * cols), jnp.float32),
+            pltpu.VMEM((8, roots, 128), jnp.float32),
+            pltpu.VMEM((4, roots, 128), jnp.float32),
+            pltpu.VMEM((nz, roots, 128), jnp.float32),
             pltpu.SemaphoreType.DMA((len(ids),)),
             pltpu.SemaphoreType.DMA((len(ids),)),
             pltpu.SemaphoreType.DMA((3,)),
         ],
         compiler_params=pltpu.CompilerParams(
-            collective_id=0, has_side_effects=True, vmem_limit_bytes=50 * 1024 * 1024),
+            collective_id=0, has_side_effects=True, vmem_limit_bytes=63 * 1024 * 1024),
     )(amplitudes, integrals, left_amps)
-    local = jnp.sum(gram, axis=2).T
     occ = rows * 8
     factor = 1.0 / math.sqrt(occ * cols * nz * 4)
-    return sigma, lax.psum(local, AXES) * factor
+    return sigma, gram[:, :roots] * factor
 
 
 def solution(mesh):

time: 161 us -> 98.5 us (0.61)
  blocking collectives: 75 us -> 0 us
  Pallas kernels: 80.7 us -> 93.9 us
  local copies, waits for them, and re-layouts: 4.75 us -> 2.27 us
    psum x1 -> x0, blocking collectives: 75 us -> none  [body(): return (sigma, lax.psum(local, AXES) * factor)]
    pallas_call x1, Pallas kernels: 80.7 us -> 93.9 us  [body(): pl.pallas_call(functools.partial(kernel, ids, nz), out_shape=(jax.ShapeDt...]
    unnamed x8 -> x1, local copies, waits for them, and re-layouts: 4.75 us -> 2.27 us
where the time goes in v2:
time: 98.5 us; the launch traced here: 98.1 us
  Pallas kernels  93.9 us (95%)
  local copies, waits for them, and re-layouts  2.27 us (2%)
  other arithmetic  1.27 us (1%)
    pallas_call x1, Pallas kernels, body(): pl.pallas_call(functools.partial(kernel, ids, nz), out_shape=(jax.ShapeDt...  93.9 us
    unnamed x1, local copies, waits for them, and re-layouts  2.27 us

profile of v2, /device:TPU:1, one launch (start us, length us, event | category | flops | bytes accessed | tf_op | source)
XLA Modules:
  0.0 98.1 jit_solution(4832945563157409173)
XLA Ops:
  0.6 93.9 %shard_map.50 = (bf16[8,512,128]{2,1,0:T(8,128)(2,1)}, f32[8,128]{1,0:T(8,128)}) custom-call(bf16[512,256]{1,0:T(8,128)(2,1)} %t2_hbm.1, bf16[512,256]{1,0:T(8,128)(2,1)} %int_hbm.1, bf16[8,512,128]{2,1,0:T(8,128)(2,1)} %left_hbm.1), custom_call_target="tpu_custom_call" | custom-call | tf_op jit(solution)/shard_map/pallas_call | solution.py:400
  94.5 1.3 %slice_multiply_fusion = f32[8,8]{1,0:T(8,128)} fusion(f32[8,128]{1,0:T(8,128)} %get-tuple-element.5), kind=kLoop, calls=%fused_computation | loop fusion | flops 64 | bytes 512 | tf_op jit(solution)/shard_map/mul | solution.py:429
  95.8 2.3 %copy.6 = bf16[8,512,128]{2,1,0:T(8,128)(2,1)} copy(bf16[8,512,128]{2,1,0:T(8,128)(2,1)} %get-tuple-element.8) | data formatting | bytes 2097152
